TPU v7x, 256 devices: a whole 4x4x8 slice. The times are simulated.
256 devices in a mesh: grp: 8 (over z), shard: 32 (over y, x, core).
Axes of the slice: x: 4, y: 4, z: 8, core: 2. Of those that a mesh axis runs over, the one named last changes fastest.
Arguments:
- table: float32 [4096, 8, 128], P('shard')
- table_first: float32 [4096, 8, 128], P('shard'), may hold values from -3 to 3
- table_second: float32 [4096, 8, 128], P('shard')
- slot_table: int32 [4096], P('shard'), may hold values from 0 to 25
- touched: int32 [8, 4096], P('grp', 'shard'), may hold values from 0 to 4095, as said below
- emb_grads: bfloat16 [8, 4096, 8, 128], P('grp', 'shard'), may hold values from -6 to 6
- block_slot: int32 [4096], replicated, may hold values from 0 to 4095, as said below
- dense_x: bfloat16 [13, 1048576], P(None, ('grp', 'shard')), may hold values from -6 to 6
- dense_cot: bfloat16 [1048576, 128], P(('grp', 'shard')), may hold values from -0.0625 to 0.0625
- w_one: float32 [13, 512], replicated, may hold values from -1.75 to 1.75
- w_two: float32 [512, 256], replicated, may hold values from -0.25 to 0.25
- w_three: float32 [256, 128], replicated, may hold values from -0.375 to 0.375
- first_one: float32 [13, 512], replicated, may hold values from -3 to 3
- first_two: float32 [512, 256], replicated, may hold values from -3 to 3
- first_three: float32 [256, 128], replicated, may hold values from -3 to 3
- second_one: float32 [13, 512], replicated, may hold values from 0.001 to 0.3
- second_two: float32 [512, 256], replicated, may hold values from 0.001 to 0.3
- second_three: float32 [256, 128], replicated, may hold values from 0.001 to 0.3
Outputs:
- new_table: float32 [4096, 8, 128], P('shard')
- new_table_first: float32 [4096, 8, 128], P('shard')
- new_table_second: float32 [4096, 8, 128], P('shard')
- new_w_one: float32 [13, 512], replicated
- new_w_two: float32 [512, 256], replicated
- new_w_three: float32 [256, 128], replicated
- new_first_one: float32 [13, 512], replicated
- new_first_two: float32 [512, 256], replicated
- new_first_three: float32 [256, 128], replicated
- new_second_one: float32 [13, 512], replicated
- new_second_two: float32 [512, 256], replicated
- new_second_three: float32 [256, 128], replicated
Inputs may be any that keep to these rules, and one draw needn't show every extreme that they name: `touched`: each device's 128 ids are distinct; at most 8 of them have block_slot // 128 equal to any one shard, and in every draw some shard gets exactly 8 from every device. `block_slot`: A permutation of the 4096 slots.
All inputs are finite; a program needn't handle non-finite values.
Results may differ from a plain program's by a relative error of at most 0.0037.
Values may be sent and summed in bfloat16 or wider, within the bound.
No kernel may reach another device: no remote copies, remote signals or barrier semaphores. Data moves between devices by JAX's collectives and lax.ppermute only.
A program may use at most 128 MiB of HBM per device.

v0:
```python
import jax
import jax.numpy as jnp
from jax import lax
from jax.sharding import Mesh
from jax.sharding import PartitionSpec as P

TABLES = 26
CAP = 8
SHARD = ("shard_0", "shard_1", "shard_2")
GRP_SHARD = ("grp", "shard_0", "shard_1", "shard_2")
beta_one = 0.9
beta_two = 0.999
corr_first = 1.0 - 0.9**10
corr_second = 1.0 - 0.999**10
adam_eps = 1e-06
decay_rate = 0.01
learn_rate = 0.1
ratio_eps = 1e-06


def rows_for(lines, count):
    spare = -lines.shape[0] % count
    if not spare:
        return lines
    return jnp.concatenate([lines, jnp.zeros((spare, *lines.shape[1:]), lines.dtype)])


def from_everyone(value, axis):
    copies = jnp.broadcast_to(value, (lax.axis_size(axis), *value.shape))
    return lax.all_to_all(copies, axis, split_axis=0, concat_axis=0, tiled=True)


def in_order(pieces, dim):
    pieces = jnp.moveaxis(pieces, 0, dim)
    shape = pieces.shape
    return pieces.reshape(*shape[:dim], shape[dim] * shape[dim + 1], *shape[dim + 2 :])


def gathered_by_axis(value, axes, dim):
    far, near = axes
    pieces = from_everyone(from_everyone(value, far), near)
    return in_order(pieces.swapaxes(0, 1).reshape(-1, *value.shape), dim)


def cut_along(value, dim, count):
    before, after = (value.shape[:dim], value.shape[dim + 1 :])
    return jnp.moveaxis(value.reshape(*before, count, -1, *after), dim, 0)


def summed_on_arrival(value, axis, dim):
    count = lax.axis_size(axis)
    pieces = lax.all_to_all(cut_along(value, dim, count), axis, 0, 0, tiled=True)
    return jnp.sum(pieces, axis=0)


def summed_rows(value, axes, dim):
    far, near = axes
    pieces = cut_along(value, dim, lax.axis_size(far))
    nearer = summed_on_arrival(pieces, near, dim + 1)
    arrived = lax.all_to_all(nearer, far, split_axis=0, concat_axis=0, tiled=True)
    return arrived.sum(axis=0)


def total_of(value, axes):
    padded = rows_for(value, lax.axis_size(axes[0]) * lax.axis_size(axes[1]))
    whole = gathered_by_axis(summed_rows(padded, axes, 0), axes, 0)
    return lax.slice_in_dim(whole, 0, len(value)).reshape(value.shape)


def packed_total(arrays, axis):
    line, at, finished = (jnp.concatenate([a.reshape(-1) for a in arrays]), 0, [])
    running = total_of(line, axis)
    for a in arrays:
        finished.append(running[at : at + a.size].reshape(a.shape))
        at += a.size
    return tuple(finished)


def silu_slope(pre_value):
    logistic = jax.nn.sigmoid(pre_value)
    return logistic * (1.0 + pre_value * (1.0 - logistic))


def tower_grads(dense_x, dense_cot, w_one, w_two, w_three):
    w_one_bf = w_one.astype(jnp.bfloat16)
    w_two_bf = w_two.astype(jnp.bfloat16)
    w_three_bf = w_three.astype(jnp.bfloat16)
    pre_one = lax.dot_general(
        dense_x, w_one_bf, (((0,), (0,)), ((), ())), preferred_element_type=jnp.float32
    )
    hidden_one = jax.nn.silu(pre_one).astype(jnp.bfloat16)
    pre_two = jnp.dot(hidden_one, w_two_bf, preferred_element_type=jnp.float32)
    hidden_two = jax.nn.silu(pre_two).astype(jnp.bfloat16)
    grad_three = lax.dot_general(
        hidden_two, dense_cot, (((0,), (0,)), ((), ())), preferred_element_type=jnp.float32
    )
    back_two = (
        lax.dot_general(
            dense_cot, w_three_bf, (((1,), (1,)), ((), ())), preferred_element_type=jnp.float32
        )
        * silu_slope(pre_two)
    ).astype(jnp.bfloat16)
    grad_two = lax.dot_general(
        hidden_one, back_two, (((0,), (0,)), ((), ())), preferred_element_type=jnp.float32
    )
    back_one = (
        lax.dot_general(
            back_two, w_two_bf, (((1,), (1,)), ((), ())), preferred_element_type=jnp.float32
        )
        * silu_slope(pre_one)
    ).astype(jnp.bfloat16)
    grad_one = jnp.dot(dense_x, back_one, preferred_element_type=jnp.float32)
    return (grad_one, grad_two, grad_three)


def lamb_dense(weight, first_in, second_in, gradient):
    first_out = beta_one * first_in + (1.0 - beta_one) * gradient
    second_out = beta_two * second_in + (1.0 - beta_two) * gradient * gradient
    update = (
        first_out / corr_first / (jnp.sqrt(second_out / corr_second) + adam_eps)
        + decay_rate * weight
    )
    trust_ratio = jnp.sqrt(jnp.sum(weight * weight)) / (
        jnp.sqrt(jnp.sum(update * update)) + ratio_eps
    )
    return (weight - learn_rate * trust_ratio * update, first_out, second_out)


def body(
    table,
    table_first,
    table_second,
    slot_table,
    touched,
    emb_grads,
    block_slot,
    dense_x,
    dense_cot,
    w_one,
    w_two,
    w_three,
    first_one,
    first_two,
    first_three,
    second_one,
    second_two,
    second_three,
):
    shards = lax.axis_size(SHARD)
    local_blocks = table.shape[0]
    block_rows = table.shape[1]
    emb_width = table.shape[2]
    row_width = block_rows * emb_width
    capacity = CAP
    dense_terms = tower_grads(dense_x, dense_cot, w_one, w_two, w_three)
    table_hot = (slot_table[:, None] == jnp.arange(TABLES, dtype=jnp.int32)[None, :]).astype(
        jnp.float32
    )
    row_weight = jnp.sum(table * table, axis=(1, 2))
    part_weight = jnp.dot(row_weight, table_hot)
    block_ids = touched[0]
    count_touched = block_ids.shape[0]
    grad_rows = emb_grads[0].reshape(count_touched, row_width)
    slot_index = jnp.take(block_slot, block_ids)
    owner_shard = slot_index // local_blocks
    local_row = slot_index % local_blocks
    owner_hot = (owner_shard[:, None] == jnp.arange(shards, dtype=jnp.int32)[None, :]).astype(
        jnp.int32
    )
    bucket_rank = jnp.cumsum(owner_hot, axis=0) - 1
    bucket_place = jnp.sum(owner_hot * bucket_rank, axis=1)
    send_index = owner_shard * capacity + bucket_place
    picker = jnp.arange(shards * capacity, dtype=jnp.int32)[:, None] == send_index[None, :]
    send_rows = jnp.dot(
        picker.astype(jnp.bfloat16), grad_rows, preferred_element_type=jnp.float32
    ).astype(jnp.bfloat16)
    send_local = jnp.where(
        jnp.any(picker, axis=1), jnp.sum(jnp.where(picker, local_row[None, :], 0), axis=1), -1
    )
    send_rows = send_rows.reshape(shards, capacity, row_width)
    send_local = send_local.reshape(shards, capacity)
    recv_rows, recv_local = (
        lax.all_to_all(send_rows, SHARD, split_axis=0, concat_axis=0, tiled=True),
        lax.all_to_all(send_local, SHARD, split_axis=0, concat_axis=0, tiled=True),
    )
    piece_rows = lax.all_gather(recv_rows, "grp", axis=0, tiled=True).reshape(-1, row_width)
    piece_locals = lax.all_gather(recv_local, "grp", axis=0, tiled=True).reshape(-1)
    matches = piece_locals[:, None] == jnp.arange(local_blocks, dtype=jnp.int32)[None, :]
    summed = lax.dot_general(
        matches.astype(jnp.bfloat16),
        piece_rows,
        (((0,), (0,)), ((), ())),
        preferred_element_type=jnp.float32,
    )
    counted = jnp.sum(matches.astype(jnp.float32), axis=0)
    emb_grad = summed.reshape(local_blocks, block_rows, emb_width)
    touched_mask = (counted > 0.5)[:, None, None]
    new_first = jnp.where(
        touched_mask, beta_one * table_first + (1.0 - beta_one) * emb_grad, table_first
    )
    new_second = jnp.where(
        touched_mask, beta_two * table_second + (1.0 - beta_two) * emb_grad * emb_grad, table_second
    )
    update = jnp.where(
        touched_mask,
        new_first / corr_first / (jnp.sqrt(new_second / corr_second) + adam_eps)
        + decay_rate * table,
        0.0,
    )
    row_update = jnp.sum(update * update, axis=(1, 2))
    part_update = jnp.dot(row_update, table_hot)
    merged = packed_total(
        (dense_terms[0], dense_terms[1], dense_terms[2], part_weight, part_update),
        (("grp", "shard_0"), ("shard_1", "shard_2")),
    )
    dense_grads = (merged[0], merged[1], merged[2])
    weight_total = merged[3] / lax.axis_size("grp")
    update_total = merged[4] / lax.axis_size("grp")
    table_ratio = jnp.sqrt(weight_total) / (jnp.sqrt(update_total) + ratio_eps)
    ratio_rows = jnp.dot(table_hot, table_ratio)
    new_table = table - learn_rate * ratio_rows[:, None, None] * update
    layer_one = lamb_dense(w_one, first_one, second_one, dense_grads[0])
    layer_two = lamb_dense(w_two, first_two, second_two, dense_grads[1])
    layer_three = lamb_dense(w_three, first_three, second_three, dense_grads[2])
    return (
        new_table,
        new_first,
        new_second,
        layer_one[0],
        layer_two[0],
        layer_three[0],
        layer_one[1],
        layer_two[1],
        layer_three[1],
        layer_one[2],
        layer_two[2],
        layer_three[2],
    )


def solution(mesh):
    finer = Mesh(
        mesh.devices.reshape(mesh.shape["grp"], 4, 4, 2), ("grp", "shard_0", "shard_1", "shard_2")
    )
    placed = (
        P(SHARD, None, None),
        P(SHARD, None, None),
        P(SHARD, None, None),
        P(SHARD),
        P("grp", SHARD),
        P("grp", SHARD, None, None),
        P(),
        P(None, GRP_SHARD),
        P(GRP_SHARD, None),
        P(),
        P(),
        P(),
        P(),
        P(),
        P(),
        P(),
        P(),
        P(),
    )
    return jax.shard_map(
        body,
        mesh=finer,
        in_specs=placed,
        out_specs=(
            P(SHARD, None, None),
            P(SHARD, None, None),
            P(SHARD, None, None),
            P(),
            P(),
            P(),
            P(),
            P(),
            P(),
            P(),
            P(),
            P(),
        ),
        check_vma=False,
    )
```

profile of v0, /device:TPU:1, one launch (start us, length us, event | category | flops | bytes accessed | tf_op | source)
XLA Modules:
  0.0 203.5 jit_solution(15515118279379365087)
XLA Ops:
  7.2 0.7 fusion.30
  8.0 1.6 gather_fusion
  9.6 0.7 and_select_fusion.1
  10.3 0.7 fusion.29
  11.4 1.2 fusion.2
  12.7 19.9 %all_to_all.42 = bf16[32,8,1024]{2,1,0:T(8,128)(2,1)} all-to-all(bf16[32,8,1024]{2,1,0:T(8,128)(2,1)S(1)} %fusion.2), channel_id=1, replica_groups=mesh['grp'=8,'shard_0'=4,'shard_1'=4,'shard_2'=2] {'shard_0','shard_1','..., dimensions={0} | all-to-all | bytes 1048576 | tf_op jit(solution)/shard_map/all_to_all | solution.py:183
  32.9 0.7 select_n.94
  33.6 3.9 %all-to-all-start = ((s32[32,1,8]{2,1,0:T(1,128)}), s32[32,1,8]{2,1,0:T(1,128)S(1)}, u32[]{:S(2)}, u32[]{:S(2)}) async-start(s32[32,1,8]{2,1,0:T(1,128)} %bitcast.11), calls=%async_computation | async-start | bytes 32768 | tf_op jit(solution)/shard_map/all_to_all | solution.py:184
  37.4 2.1 %multiply_reduce_fusion.3 = bf16[128]{0:T(256)(128)(2,1)S(1)} fusion(f32[128,8,128]{2,1,0:T(8,128)} %param.18), kind=kLoop, calls=%fused_computation.37 | loop fusion | flops 262016 | bytes 524544 | tf_op jit(solution)/shard_map/reduce_sum | solution.py:159
  39.5 6.6 %multiply_convert_fusion.1 = (bf16[4096,512]{1,0:T(8,128)(2,1)S(1)}, f32[4096,512]{1,0:T(8,128)}) fusion(bf16[13,4096]{1,0:T(8,128)(2,1)} %param.25, f32[13,512]{1,0:T(8,128)} %param.27), kind=kOutput, calls=%fused_computation.2 | convolution fusion | flops 65018368 | bytes 12716032 | tf_op jit(solution)/shard_map/dot_general | solution.py:88
  46.1 1.3 fusion.18
  47.4 1.7 fusion
  49.1 2.1 %convolution_bitcast_fusion.1 = f32[64,2,8,128]{3,2,1,0:T(8,128)} fusion(bf16[4096,512]{1,0:T(8,128)(2,1)S(1)} %get-tuple-element.102, bf16[4096,256]{1,0:T(8,128)(2,1)S(1)} %fusion), kind=kOutput, calls=%fused_computation.12 | convolution fusion | flops 1073741824 | bytes 6815744 | tf_op jit(solution)/shard_map/dot_general | solution.py:103
  51.2 1.3 convolution_bitcast_fusion
  52.5 7.6 %fusion.3 = f32[13,512]{1,0:T(8,128)S(1)} fusion(bf16[13,4096]{1,0:T(8,128)(2,1)S(1)} %copy-done.18, f32[4096,512]{1,0:T(8,128)} %get-tuple-element.103, bf16[4096,256]{1,0:T(8,128)(2,1)} %copy-done.20, f32[512,256]{1,0:T(8,128)S(1)} %copy-done.1), kind=kOutput, calls=%fused_computation.13 | convolution fusion | flops 1147273216 | bytes 11143168 | tf_op jit(solution)/shard_map/dot_general | solution.py:112
  60.4 0.4 copy.100
  60.8 1.0 copy.92
  61.9 2.0 %copy.95 = f32[128,8,128]{0,2,1:T(8,128)} copy(f32[128,8,128]{2,1,0:T(8,128)} %param.20) | data formatting | bytes 1048576 | tf_op args[2]
  63.9 1.3 copy.107
  65.2 24.8 %all-gather = s32[256,1,8]{2,1,0:T(1,128)S(1)} all-gather(s32[32,1,8]{2,1,0:T(1,128)S(1)} %all-to-all-done), channel_id=2, replica_groups=mesh['grp'=8,'shard_0'=4,'shard_1'=4,'shard_2'=2] {'grp'}, dimensions={0}, use_global_device_ids=true | all-gather | bytes 9216 | tf_op jit(solution)/shard_map/all_gather | solution.py:187
  90.1 0.5 broadcast.181
  90.6 1.0 reduce.4
  92.1 6.6 %copy.93 = bf16[2048,1024]{0,1:T(8,128)(2,1)} copy(bf16[2048,1024]{1,0:T(8,128)(2,1)} %bitcast.74) | data formatting | bytes 8388608 | tf_op jit(solution)/shard_map/reshape | solution.py:186
  98.6 5.1 %multiply_reduce_fusion.2 = (bf16[128]{0:T(256)(128)(2,1)S(1)}, f32[128,8,128]{0,2,1:T(8,128)}, f32[128,8,128]{0,2,1:T(8,128)}, f32[128,8,128]{0,2,1:T(8,128)}) fusion(f32[128,8,128]{0,2,1:T(8,128)S(1)} %copy.100, pred[128]{0:T(512)(128)(4,1)S(1)} %broadcast_compare_fusion, f32[128,8,128]{0,2,1:T(8,128)S(1)} %copy-done.9, f32[128,8,128]{0,2,1:T(8,128)} %copy.95, ...), kind=kOutput, calls=%fused_computation.33 | convolution fusion | flops 539492224 | bytes 7348608 | tf_op jit(solution)/shard_map/dot_general | solution.py:189
  103.9 2.8 %concatenate.3 = f32[170752]{0:T(1024)S(1)} concatenate(f32[6656]{0:T(1024)S(1)} %reshape.152, f32[131072]{0:T(1024)S(1)} %bitcast.78, f32[32768]{0:T(1024)S(1)} %convolution_bitcast_fusion, f32[26]{0:T(128)S(1)} %convolution_bitcast_fusion.4, f32[26]{0:T(128)S(1)} %convolution_bitcast_fusion.3, f32[204]{0:T(256)S(1)} %broadcast_in_dim.74), dimensions={0} | concatenate | bytes 1366016 | tf_op jit(solution)/shard_map/concatenate | solution.py:25
  106.7 0.7 reshape_reshape.6
  107.7 21.0 %all_to_all.43 = f32[8,32,667]{2,1,0:T(8,128)S(1)} all-to-all(f32[8,32,667]{2,1,0:T(8,128)S(1)} %copy.98), channel_id=1, replica_groups=mesh['grp'=8,'shard_0'=4,'shard_1'=4,'shard_2'=2] {'shard_1','shard_2'}, dimensions={0} | all-to-all | bytes 1366016 | tf_op jit(solution)/shard_map/all_to_all | solution.py:52
  128.8 0.7 reduce_sum.125
  129.4 1.0 all_to_all.31
  130.4 16.4 %all_to_all.44 = f32[32,1,667]{2,1,0:T(1,128)S(1)} all-to-all(f32[32,1,667]{2,1,0:T(1,128)S(1)} %all_to_all.31), channel_id=1, replica_groups=mesh['grp'=8,'shard_0'=4,'shard_1'=4,'shard_2'=2] {'grp','shard_0'}, dimensions={0} | all-to-all | bytes 170752 | tf_op jit(solution)/shard_map/all_to_all | solution.py:60
  147.0 12.3 %all_to_all.45 = f32[32,1,667]{2,1,0:T(1,128)S(1)} all-to-all(f32[32,1,667]{2,1,0:T(1,128)S(1)} %broadcast_in_dim.75), channel_id=1, replica_groups=mesh['grp'=8,'shard_0'=4,'shard_1'=4,'shard_2'=2] {'grp','shard_0'}, dimensions={0} | all-to-all | bytes 170752 | tf_op jit(solution)/shard_map/all_to_all | solution.py:30
  159.3 0.9 broadcast_in_dim.76
  160.2 7.1 %all-to-all-start.5 = ((f32[8,32,667]{2,1,0:T(8,128)}), f32[8,32,667]{2,1,0:T(8,128)S(1)}, u32[]{:S(2)}, u32[]{:S(2)}) async-start(f32[8,32,667]{2,1,0:T(8,128)} %broadcast_in_dim.76), calls=%async_computation.5 | async-start | bytes 1572864 | tf_op jit(solution)/shard_map/all_to_all | solution.py:30
  167.3 1.0 copy.104
  168.3 1.0 copy.105
  169.3 10.2 %all-to-all-done.5 = f32[8,32,667]{2,1,0:T(8,128)S(1)} async-done(((f32[8,32,667]{2,1,0:T(8,128)}), f32[8,32,667]{2,1,0:T(8,128)S(1)}, u32[]{:S(2)}, u32[]{:S(2)}) %all-to-all-start.5) | async-done | bytes 683040 | tf_op jit(solution)/shard_map/all_to_all | solution.py:30
  179.5 0.5 copy.99
  180.0 0.5 reshape_reshape.7
  180.7 0.8 slice.30
  181.5 1.4 slice.32
  182.9 1.3 multiply_subtract_fusion.1
  184.1 1.0 copy.103
  185.2 0.6 multiply_reduce_fusion.6
  187.2 2.3 %multiply_reduce_fusion = (f32[]{:T(128)}, f32[]{:T(128)}, f32[512,256]{1,0:T(8,128)S(1)}, f32[512,256]{1,0:T(8,128)S(1)}) fusion(f32[512,256]{1,0:T(8,128)S(1)} %copy-done.1, f32[667,256]{1,0:T(8,128)S(1)} %slice.30, f32[512,256]{1,0:T(8,128)} %param.31, f32[512,256]{1,0:T(8,128)} %param.34), kind=kLoop, calls=%fused_computation.28 | loop fusion | flops 2228222 | bytes 3145736 | tf_op jit(solution)/shard_map/reduce_sum | solution.py:124
  190.9 1.8 multiply_reduce_fusion.4
  194.1 0.6 multiply_subtract_fusion.3
  194.8 1.1 multiply_subtract_fusion
  195.9 0.7 multiply_subtract_fusion.2
  (68 shorter events, 2.4 us)
Async XLA Ops:
  7.2 40.2 %copy-start = (bf16[4096,128]{1,0:T(8,128)(2,1)S(1)}, bf16[4096,128]{1,0:T(8,128)(2,1)}, u32[]{:S(2)}) copy-start(bf16[4096,128]{1,0:T(8,128)(2,1)} %param.26) | copy-start | bytes 3145732
  7.2 84.8 %all-gather.3.cloned.1.call-start = ((), (), s32[]{:S(2)}) async-start(), calls=%async_computation.6 | async-start | bytes 4718592 | tf_op jit(solution)/shard_map/all_gather | solution.py:186
  33.6 31.7 %all-to-all-start = ((s32[32,1,8]{2,1,0:T(1,128)}), s32[32,1,8]{2,1,0:T(1,128)S(1)}, u32[]{:S(2)}, u32[]{:S(2)}) async-start(s32[32,1,8]{2,1,0:T(1,128)} %bitcast.11), calls=%async_computation | async-start | bytes 32768 | tf_op jit(solution)/shard_map/all_to_all | solution.py:184
  39.5 6.6 %copy-start.1 = (f32[512,256]{1,0:T(8,128)S(1)}, f32[512,256]{1,0:T(8,128)}, u32[]{:S(2)}) copy-start(f32[512,256]{1,0:T(8,128)} %param.28) | copy-start | bytes 1572868
  46.1 1.3 copy-start.10
  49.1 2.1 %copy-start.20 = (bf16[4096,256]{1,0:T(8,128)(2,1)}, bf16[4096,256]{1,0:T(8,128)(2,1)S(1)}, u32[]{:S(2)}) copy-start(bf16[4096,256]{1,0:T(8,128)(2,1)S(1)} %fusion) | copy-start | bytes 6291460
  51.2 1.3 copy-start.18
  52.5 7.7 %copy-start.19 = (s32[128]{0:T(128)S(1)}, s32[128]{0:T(128)}, u32[]{:S(2)}) copy-start(s32[128]{0:T(128)} %param.21) | copy-start | bytes 1540
  52.5 7.9 %copy-start.2 = (f32[128,8,128]{2,1,0:T(8,128)S(1)}, f32[128,8,128]{2,1,0:T(8,128)}, u32[]{:S(2)}) copy-start(f32[128,8,128]{2,1,0:T(8,128)} %param.18) | copy-start | bytes 1572868
  52.5 8.3 %copy-start.6 = (f32[128,8,128]{2,1,0:T(8,128)S(1)}, f32[128,8,128]{2,1,0:T(8,128)}, u32[]{:S(2)}) copy-start(f32[128,8,128]{2,1,0:T(8,128)} %param.19) | copy-start | bytes 1572868
  60.8 37.8 %copy-start.3 = (f32[128,8,128]{0,2,1:T(8,128)}, f32[128,8,128]{0,2,1:T(8,128)S(1)}, u32[]{:S(2)}) copy-start(f32[128,8,128]{0,2,1:T(8,128)S(1)} %copy.100) | copy-start | bytes 1572868
  92.0 6.6 %copy-start.9 = (f32[128,8,128]{0,2,1:T(8,128)S(1)}, f32[128,8,128]{0,2,1:T(8,128)}, u32[]{:S(2)}) copy-start(f32[128,8,128]{0,2,1:T(8,128)} %copy.92) | copy-start | bytes 1572868
  107.4 59.9 %copy-start.8 = (f32[128,8,128]{0,2,1:T(8,128)S(1)}, f32[128,8,128]{0,2,1:T(8,128)}, u32[]{:S(2)}) copy-start(f32[128,8,128]{0,2,1:T(8,128)} %get-tuple-element.98) | copy-start | bytes 1572868
  107.4 60.9 %copy-start.7 = (f32[128,8,128]{0,2,1:T(8,128)S(1)}, f32[128,8,128]{0,2,1:T(8,128)}, u32[]{:S(2)}) copy-start(f32[128,8,128]{0,2,1:T(8,128)} %get-tuple-element.99) | copy-start | bytes 1572868
  160.2 19.3 %all-to-all-start.5 = ((f32[8,32,667]{2,1,0:T(8,128)}), f32[8,32,667]{2,1,0:T(8,128)S(1)}, u32[]{:S(2)}, u32[]{:S(2)}) async-start(f32[8,32,667]{2,1,0:T(8,128)} %broadcast_in_dim.76), calls=%async_computation.5 | async-start | bytes 1572864 | tf_op jit(solution)/shard_map/all_to_all | solution.py:30
  179.5 5.6 %copy-start.13 = (f32[13,512]{1,0:T(8,128)S(1)}, f32[13,512]{1,0:T(8,128)}, u32[]{:S(2)}) copy-start(f32[13,512]{1,0:T(8,128)} %param.27) | copy-start | bytes 79876
  179.5 5.6 %copy-start.16 = (f32[13,512]{1,0:T(8,128)S(1)}, f32[13,512]{1,0:T(8,128)}, u32[]{:S(2)}) copy-start(f32[13,512]{1,0:T(8,128)} %param.30) | copy-start | bytes 79876
  179.5 5.6 %copy-start.17 = (f32[13,512]{1,0:T(8,128)S(1)}, f32[13,512]{1,0:T(8,128)}, u32[]{:S(2)}) copy-start(f32[13,512]{1,0:T(8,128)} %param.33) | copy-start | bytes 79876
  185.8 10.8 %copy-start.14 = (f32[13,512]{1,0:T(8,128)}, f32[13,512]{1,0:T(8,128)S(1)}, u32[]{:S(2)}) copy-start(f32[13,512]{1,0:T(8,128)S(1)} %get-tuple-element.94) | copy-start | bytes 79876
  185.8 10.8 %copy-start.15 = (f32[13,512]{1,0:T(8,128)}, f32[13,512]{1,0:T(8,128)S(1)}, u32[]{:S(2)}) copy-start(f32[13,512]{1,0:T(8,128)S(1)} %get-tuple-element.95) | copy-start | bytes 79876
  189.5 7.1 %copy-start.4 = (f32[512,256]{1,0:T(8,128)}, f32[512,256]{1,0:T(8,128)S(1)}, u32[]{:S(2)}) copy-start(f32[512,256]{1,0:T(8,128)S(1)} %get-tuple-element.92) | copy-start | bytes 1572868
  189.5 7.1 %copy-start.5 = (f32[512,256]{1,0:T(8,128)}, f32[512,256]{1,0:T(8,128)S(1)}, u32[]{:S(2)}) copy-start(f32[512,256]{1,0:T(8,128)S(1)} %get-tuple-element.93) | copy-start | bytes 1572868
  192.7 3.9 %copy-start.11 = (f32[256,128]{1,0:T(8,128)}, f32[256,128]{1,0:T(8,128)S(1)}, u32[]{:S(2)}) copy-start(f32[256,128]{1,0:T(8,128)S(1)} %get-tuple-element.90) | copy-start | bytes 393220
  192.7 3.9 %copy-start.12 = (f32[256,128]{1,0:T(8,128)}, f32[256,128]{1,0:T(8,128)S(1)}, u32[]{:S(2)}) copy-start(f32[256,128]{1,0:T(8,128)S(1)} %get-tuple-element.91) | copy-start | bytes 393220
Sparse Core Ops, SparseCore 0:
  32.7 54.4 all-gather.2
where the time goes:
time: 204 us; the launch traced here: 203 us
  blocking collectives  94.5 us (46%)
  matrix products  27.5 us (13%)
  local copies, waits for them, and re-layouts  26.3 us (13%)
  between operations  18.6 us (9%)
  other arithmetic  15.3 us (8%)
  starting transfers between devices  11 us (5%)
  waiting for transfers between devices  10.2 us (5%)
    all_gather x1, blocking collectives, body(): lax.all_gather(recv_local, 'grp', axis=0, tiled=True).reshape(-1)  24.8 us
    all_to_all x1, blocking collectives, summed_on_arrival(): lax.all_to_all(cut_along(value, dim, count), axis, 0, 0, tiled=True)  21 us
    all_to_all x1, blocking collectives, body(): lax.all_to_all(send_rows, SHARD, split_axis=0, concat_axis=0, tiled=True)  19.9 us
    all_to_all x1, blocking collectives, summed_rows(): lax.all_to_all(nearer, far, split_axis=0, concat_axis=0, tiled=True)  16.4 us
    all_to_all x1, blocking collectives, from_everyone(): return lax.all_to_all(copies, axis, split_axis=0, concat_axis=0, tiled=True)  12.3 us
    all_to_all x1, waiting for transfers between devices, from_everyone(): return lax.all_to_all(copies, axis, split_axis=0, concat_axis=0, tiled=True)  10.2 us
    unnamed x50, local copies, waits for them, and re-layouts  7.89 us
    dot_general x1, matrix products, tower_grads(): grad_one = jnp.dot(dense_x, back_one, preferred_element_type=jnp.float32)  7.65 us
  transfers between devices with their start and end apart: 3, of which 1 were waited for; matrix products, arithmetic and copies ran while one was open for 16% of the time, Pallas kernels for 0%

commit v1 on v0

--- a/solution.py
+++ b/solution.py
@@ -16,6 +16,12 @@
 decay_rate = 0.01
 learn_rate = 0.1
 ratio_eps = 1e-06
+
+
+def choose_sections(slab_in):
+    lower = jnp.concatenate(lax.axis_size("grp") * [slab_in], axis=0)
+    r2 = lax.all_to_all(lower, axis_name="grp", split_axis=0, concat_axis=0, tiled=True)
+    return r2
 
 
 def rows_for(lines, count):
@@ -184,7 +190,7 @@
         lax.all_to_all(send_local, SHARD, split_axis=0, concat_axis=0, tiled=True),
     )
     piece_rows = lax.all_gather(recv_rows, "grp", axis=0, tiled=True).reshape(-1, row_width)
-    piece_locals = lax.all_gather(recv_local, "grp", axis=0, tiled=True).reshape(-1)
+    piece_locals = choose_sections(recv_local).reshape(-1)
     matches = piece_locals[:, None] == jnp.arange(local_blocks, dtype=jnp.int32)[None, :]
     summed = lax.dot_general(
         matches.astype(jnp.bfloat16),

time: 204 us -> 194 us (0.951)
  blocking collectives: 94.5 us -> 65.1 us
  waiting for transfers between devices: 10.2 us -> 21.8 us
  starting transfers between devices: 11 us -> 19.2 us
    all_gather x1 -> x0, blocking collectives: 24.8 us -> none  [body(): lax.all_gather(recv_local, 'grp', axis=0, tiled=True).reshape(-1)]
    all_gather x1, waiting for transfers between devices: 0.02 us -> 9.57 us  [body(): lax.all_gather(recv_rows, 'grp', axis=0, tiled=True).reshape(-1, row_width)]
    all_to_all x0 -> x1, starting transfers between devices: none -> 8.19 us  [choose_sections(): lax.all_to_all(lower, axis_name='grp', split_axis=0, concat_axis=0, tiled...]
    all_to_all x1, blocking collectives: 21 us -> 17.1 us  [summed_on_arrival(): lax.all_to_all(cut_along(value, dim, count), axis, 0, 0, tiled=True)]
    all_to_all x0 -> x1, waiting for transfers between devices: none -> 2.06 us  [choose_sections(): lax.all_to_all(lower, axis_name='grp', split_axis=0, concat_axis=0, tiled...]
    unnamed x50 -> x52, local copies, waits for them, and re-layouts: 7.89 us -> 8.47 us
  transfers between devices with their start and end apart: 3 -> 4, of which waited for: 1 -> 3; matrix products, arithmetic and copies ran while one was open for 16% -> 17% of each run, Pallas kernels for 0% -> 0%
where the time goes in v1:
time: 194 us; the launch traced here: 193 us
  blocking collectives  65.1 us (34%)
  matrix products  27.4 us (14%)
  local copies, waits for them, and re-layouts  27.2 us (14%)
  waiting for transfers between devices  21.8 us (11%)
  starting transfers between devices  19.2 us (10%)
  between operations  18.7 us (10%)
  other arithmetic  14 us (7%)
    all_to_all x1, blocking collectives, body(): lax.all_to_all(send_rows, SHARD, split_axis=0, concat_axis=0, tiled=True)  19.9 us
    all_to_all x1, blocking collectives, summed_on_arrival(): lax.all_to_all(cut_along(value, dim, count), axis, 0, 0, tiled=True)  17.1 us
    all_to_all x1, blocking collectives, summed_rows(): lax.all_to_all(nearer, far, split_axis=0, concat_axis=0, tiled=True)  15.8 us
    all_to_all x1, blocking collectives, from_everyone(): return lax.all_to_all(copies, axis, split_axis=0, concat_axis=0, tiled=True)  12.3 us
    all_to_all x1, waiting for transfers between devices, from_everyone(): return lax.all_to_all(copies, axis, split_axis=0, concat_axis=0, tiled=True)  10.2 us
    all_gather x1, waiting for transfers between devices, body(): lax.all_gather(recv_rows, 'grp', axis=0, tiled=True).reshape(-1, row_width)  9.57 us
    unnamed x52, local copies, waits for them, and re-layouts  8.47 us
    all_to_all x1, starting transfers between devices, choose_sections(): lax.all_to_all(lower, axis_name='grp', split_axis=0, concat_axis=0, tiled...  8.19 us
  transfers between devices with their start and end apart: 4, of which 3 were waited for; matrix products, arithmetic and copies ran while one was open for 17% of the time, Pallas kernels for 0%

profile of v1, /device:TPU:1, one launch (start us, length us, event | category | flops | bytes accessed | tf_op | source)
XLA Modules:
  0.0 193.5 jit_solution(2838776021830047038)
XLA Ops:
  7.2 0.7 fusion.30
  8.0 1.6 gather_fusion
  9.6 0.7 and_select_fusion.1
  10.3 0.7 fusion.29
  11.4 1.2 fusion.2
  12.7 19.9 %all_to_all.51 = bf16[32,8,1024]{2,1,0:T(8,128)(2,1)} all-to-all(bf16[32,8,1024]{2,1,0:T(8,128)(2,1)S(1)} %fusion.2), channel_id=1, replica_groups=mesh['grp'=8,'shard_0'=4,'shard_1'=4,'shard_2'=2] {'shard_0','shard_1','..., dimensions={0} | all-to-all | bytes 1048576 | tf_op jit(solution)/shard_map/all_to_all | solution.py:189
  32.9 0.7 select_n.94
  33.6 3.9 %all-to-all-start = ((s32[32,1,8]{2,1,0:T(1,128)}), s32[32,1,8]{2,1,0:T(1,128)S(1)}, u32[]{:S(2)}, u32[]{:S(2)}) async-start(s32[32,1,8]{2,1,0:T(1,128)} %bitcast.11), calls=%async_computation | async-start | bytes 32768 | tf_op jit(solution)/shard_map/all_to_all | solution.py:190
  37.5 6.6 %multiply_convert_fusion.1 = (bf16[4096,512]{1,0:T(8,128)(2,1)S(1)}, f32[4096,512]{1,0:T(8,128)}) fusion(bf16[13,4096]{1,0:T(8,128)(2,1)} %param.25, f32[13,512]{1,0:T(8,128)} %param.27), kind=kOutput, calls=%fused_computation.2 | convolution fusion | flops 65018368 | bytes 12716032 | tf_op jit(solution)/shard_map/dot_general | solution.py:94
  44.0 1.3 fusion.18
  45.3 1.7 fusion
  47.0 2.1 %convolution_bitcast_fusion.1 = f32[64,2,8,128]{3,2,1,0:T(8,128)} fusion(bf16[4096,512]{1,0:T(8,128)(2,1)S(1)} %get-tuple-element.90, bf16[4096,256]{1,0:T(8,128)(2,1)S(1)} %fusion), kind=kOutput, calls=%fused_computation.12 | convolution fusion | flops 1073741824 | bytes 6815744 | tf_op jit(solution)/shard_map/dot_general | solution.py:109
  49.1 1.3 convolution_bitcast_fusion
  50.5 7.6 %fusion.3 = f32[13,512]{1,0:T(8,128)S(1)} fusion(bf16[13,4096]{1,0:T(8,128)(2,1)S(1)} %copy-done.18, f32[4096,512]{1,0:T(8,128)} %get-tuple-element.91, bf16[4096,256]{1,0:T(8,128)(2,1)} %copy-done.20, f32[512,256]{1,0:T(8,128)S(1)} %copy-done.1), kind=kOutput, calls=%fused_computation.13 | convolution fusion | flops 1147273216 | bytes 11143168 | tf_op jit(solution)/shard_map/dot_general | solution.py:118
  58.1 1.0 multiply_reduce_fusion.3
  59.4 0.7 reshape.176
  60.1 8.2 %all-to-all-start.1 = ((s32[8,1,256]{2,1,0:T(1,128)}), s32[8,1,256]{2,1,0:T(1,128)S(1)}, u32[]{:S(2)}, u32[]{:S(2)}) async-start(s32[8,1,256]{2,1,0:T(1,128)} %reshape.176), calls=%async_computation.1 | async-start | bytes 16384 | tf_op jit(solution)/shard_map/all_to_all | solution.py:23
  68.7 1.0 copy.106
  69.8 2.0 %copy.109 = f32[128,8,128]{0,2,1:T(8,128)} copy(f32[128,8,128]{2,1,0:T(8,128)} %param.20) | data formatting | bytes 1048576 | tf_op args[2]
  71.8 1.3 copy.121
  73.1 2.1 %all-to-all-done.1 = s32[8,1,256]{2,1,0:T(1,128)S(1)} async-done(((s32[8,1,256]{2,1,0:T(1,128)}), s32[8,1,256]{2,1,0:T(1,128)S(1)}, u32[]{:S(2)}, u32[]{:S(2)}) %all-to-all-start.1) | async-done | bytes 8224 | tf_op jit(solution)/shard_map/all_to_all | solution.py:23
  75.7 0.7 reduce.1
  77.0 9.6 %all-gather.2.cloned.1.call-done = bf16[256,8,1024]{2,1,0:T(8,128)(2,1)} async-done(((bf16[32,8,1024]{2,1,0:T(8,128)(2,1)}), bf16[256,8,1024]{2,1,0:T(8,128)(2,1)}) %all-gather.2.cloned.1.call-update) | async-done | bytes 4194320 | tf_op jit(solution)/shard_map/all_gather | solution.py:192
  86.6 6.6 %copy.107 = bf16[2048,1024]{0,1:T(8,128)(2,1)} copy(bf16[2048,1024]{1,0:T(8,128)(2,1)} %bitcast.81) | data formatting | bytes 8388608 | tf_op jit(solution)/shard_map/reshape | solution.py:192
  93.2 5.1 %multiply_reduce_fusion.2 = (bf16[128]{0:T(256)(128)(2,1)S(1)}, f32[128,8,128]{0,2,1:T(8,128)}, f32[128,8,128]{0,2,1:T(8,128)}, f32[128,8,128]{0,2,1:T(8,128)}) fusion(f32[128,8,128]{0,2,1:T(8,128)S(1)} %copy.114, pred[128]{0:T(512)(128)(4,1)S(1)} %broadcast_compare_fusion, f32[128,8,128]{0,2,1:T(8,128)S(1)} %copy-done.9, f32[128,8,128]{0,2,1:T(8,128)} %copy.109, ...), kind=kOutput, calls=%fused_computation.33 | convolution fusion | flops 539492224 | bytes 7348608 | tf_op jit(solution)/shard_map/dot_general | solution.py:195
  98.4 2.8 %concatenate.7 = f32[170752]{0:T(1024)S(1)} concatenate(f32[6656]{0:T(1024)S(1)} %reshape.155, f32[131072]{0:T(1024)S(1)} %bitcast.85, f32[32768]{0:T(1024)S(1)} %convolution_bitcast_fusion, f32[26]{0:T(128)S(1)} %convolution_bitcast_fusion.4, f32[26]{0:T(128)S(1)} %convolution_bitcast_fusion.3, f32[204]{0:T(256)S(1)} %broadcast_in_dim.74), dimensions={0} | concatenate | bytes 1366016 | tf_op jit(solution)/shard_map/concatenate | solution.py:31
  101.2 0.7 reshape_reshape.6
  102.2 17.1 %all_to_all.52 = f32[8,32,667]{2,1,0:T(8,128)S(1)} all-to-all(f32[8,32,667]{2,1,0:T(8,128)S(1)} %copy.112), channel_id=1, replica_groups=mesh['grp'=8,'shard_0'=4,'shard_1'=4,'shard_2'=2] {'shard_1','shard_2'}, dimensions={0} | all-to-all | bytes 1366016 | tf_op jit(solution)/shard_map/all_to_all | solution.py:58
  119.4 0.7 reduce_sum.125
  120.1 1.0 all_to_all.39
  121.0 15.8 %all_to_all.53 = f32[32,1,667]{2,1,0:T(1,128)S(1)} all-to-all(f32[32,1,667]{2,1,0:T(1,128)S(1)} %all_to_all.39), channel_id=1, replica_groups=mesh['grp'=8,'shard_0'=4,'shard_1'=4,'shard_2'=2] {'grp','shard_0'}, dimensions={0} | all-to-all | bytes 170752 | tf_op jit(solution)/shard_map/all_to_all | solution.py:66
  136.9 12.3 %all_to_all.54 = f32[32,1,667]{2,1,0:T(1,128)S(1)} all-to-all(f32[32,1,667]{2,1,0:T(1,128)S(1)} %broadcast_in_dim.75), channel_id=1, replica_groups=mesh['grp'=8,'shard_0'=4,'shard_1'=4,'shard_2'=2] {'grp','shard_0'}, dimensions={0} | all-to-all | bytes 170752 | tf_op jit(solution)/shard_map/all_to_all | solution.py:36
  149.3 0.9 broadcast_in_dim.76
  150.2 7.1 %all-to-all-start.6 = ((f32[8,32,667]{2,1,0:T(8,128)}), f32[8,32,667]{2,1,0:T(8,128)S(1)}, u32[]{:S(2)}, u32[]{:S(2)}) async-start(f32[8,32,667]{2,1,0:T(8,128)} %broadcast_in_dim.76), calls=%async_computation.6 | async-start | bytes 1572864 | tf_op jit(solution)/shard_map/all_to_all | solution.py:36
  157.3 1.0 copy.118
  158.3 1.0 copy.119
  159.3 10.2 %all-to-all-done.6 = f32[8,32,667]{2,1,0:T(8,128)S(1)} async-done(((f32[8,32,667]{2,1,0:T(8,128)}), f32[8,32,667]{2,1,0:T(8,128)S(1)}, u32[]{:S(2)}, u32[]{:S(2)}) %all-to-all-start.6) | async-done | bytes 683040 | tf_op jit(solution)/shard_map/all_to_all | solution.py:36
  169.9 0.5 reshape_reshape.7
  170.7 0.8 slice.30
  171.5 1.4 slice.32
  172.8 1.3 multiply_subtract_fusion.1
  174.1 1.0 copy.117
  175.1 0.6 multiply_reduce_fusion.6
  177.2 2.3 %multiply_reduce_fusion = (f32[]{:T(128)}, f32[]{:T(128)}, f32[512,256]{1,0:T(8,128)S(1)}, f32[512,256]{1,0:T(8,128)S(1)}) fusion(f32[512,256]{1,0:T(8,128)S(1)} %copy-done.1, f32[667,256]{1,0:T(8,128)S(1)} %slice.30, f32[512,256]{1,0:T(8,128)} %param.31, f32[512,256]{1,0:T(8,128)} %param.34), kind=kLoop, calls=%fused_computation.28 | loop fusion | flops 2228222 | bytes 3145736 | tf_op jit(solution)/shard_map/reduce_sum | solution.py:130
  180.9 1.8 multiply_reduce_fusion.4
  184.1 0.6 multiply_subtract_fusion.3
  184.8 1.1 multiply_subtract_fusion
  185.8 0.7 multiply_subtract_fusion.2
  (76 shorter events, 3.9 us)
Async XLA Ops:
  7.2 38.1 %copy-start = (bf16[4096,128]{1,0:T(8,128)(2,1)S(1)}, bf16[4096,128]{1,0:T(8,128)(2,1)}, u32[]{:S(2)}) copy-start(bf16[4096,128]{1,0:T(8,128)(2,1)} %param.26) | copy-start | bytes 3145732
  7.2 79.4 %all-gather.2.cloned.1.call-start = ((), (), s32[]{:S(2)}) async-start(), calls=%async_computation.7 | async-start | bytes 4718592 | tf_op jit(solution)/shard_map/all_gather | solution.py:192
  33.6 25.6 %all-to-all-start = ((s32[32,1,8]{2,1,0:T(1,128)}), s32[32,1,8]{2,1,0:T(1,128)S(1)}, u32[]{:S(2)}, u32[]{:S(2)}) async-start(s32[32,1,8]{2,1,0:T(1,128)} %bitcast.11), calls=%async_computation | async-start | bytes 32768 | tf_op jit(solution)/shard_map/all_to_all | solution.py:190
  37.4 6.6 %copy-start.1 = (f32[512,256]{1,0:T(8,128)S(1)}, f32[512,256]{1,0:T(8,128)}, u32[]{:S(2)}) copy-start(f32[512,256]{1,0:T(8,128)} %param.28) | copy-start | bytes 1572868
  44.0 1.3 copy-start.10
  47.0 2.1 %copy-start.20 = (bf16[4096,256]{1,0:T(8,128)(2,1)}, bf16[4096,256]{1,0:T(8,128)(2,1)S(1)}, u32[]{:S(2)}) copy-start(bf16[4096,256]{1,0:T(8,128)(2,1)S(1)} %fusion) | copy-start | bytes 6291460
  49.1 1.3 copy-start.18
  50.4 7.7 %copy-start.2 = (f32[128,8,128]{2,1,0:T(8,128)S(1)}, f32[128,8,128]{2,1,0:T(8,128)}, u32[]{:S(2)}) copy-start(f32[128,8,128]{2,1,0:T(8,128)} %param.18) | copy-start | bytes 1572868
  50.5 17.8 %copy-start.19 = (s32[128]{0:T(128)S(1)}, s32[128]{0:T(128)}, u32[]{:S(2)}) copy-start(s32[128]{0:T(128)} %param.21) | copy-start | bytes 1540
  50.5 18.2 %copy-start.6 = (f32[128,8,128]{2,1,0:T(8,128)S(1)}, f32[128,8,128]{2,1,0:T(8,128)}, u32[]{:S(2)}) copy-start(f32[128,8,128]{2,1,0:T(8,128)} %param.19) | copy-start | bytes 1572868
  60.1 15.1 %all-to-all-start.1 = ((s32[8,1,256]{2,1,0:T(1,128)}), s32[8,1,256]{2,1,0:T(1,128)S(1)}, u32[]{:S(2)}, u32[]{:S(2)}) async-start(s32[8,1,256]{2,1,0:T(1,128)} %reshape.176), calls=%async_computation.1 | async-start | bytes 16384 | tf_op jit(solution)/shard_map/all_to_all | solution.py:23
  68.7 24.4 %copy-start.3 = (f32[128,8,128]{0,2,1:T(8,128)}, f32[128,8,128]{0,2,1:T(8,128)S(1)}, u32[]{:S(2)}) copy-start(f32[128,8,128]{0,2,1:T(8,128)S(1)} %copy.114) | copy-start | bytes 1572868
  86.6 6.6 %copy-start.9 = (f32[128,8,128]{0,2,1:T(8,128)S(1)}, f32[128,8,128]{0,2,1:T(8,128)}, u32[]{:S(2)}) copy-start(f32[128,8,128]{0,2,1:T(8,128)} %copy.106) | copy-start | bytes 1572868
  102.0 55.3 %copy-start.8 = (f32[128,8,128]{0,2,1:T(8,128)S(1)}, f32[128,8,128]{0,2,1:T(8,128)}, u32[]{:S(2)}) copy-start(f32[128,8,128]{0,2,1:T(8,128)} %get-tuple-element.86) | copy-start | bytes 1572868
  102.0 56.3 %copy-start.7 = (f32[128,8,128]{0,2,1:T(8,128)S(1)}, f32[128,8,128]{0,2,1:T(8,128)}, u32[]{:S(2)}) copy-start(f32[128,8,128]{0,2,1:T(8,128)} %get-tuple-element.87) | copy-start | bytes 1572868
  150.2 19.3 %all-to-all-start.6 = ((f32[8,32,667]{2,1,0:T(8,128)}), f32[8,32,667]{2,1,0:T(8,128)S(1)}, u32[]{:S(2)}, u32[]{:S(2)}) async-start(f32[8,32,667]{2,1,0:T(8,128)} %broadcast_in_dim.76), calls=%async_computation.6 | async-start | bytes 1572864 | tf_op jit(solution)/shard_map/all_to_all | solution.py:36
  169.5 5.6 %copy-start.13 = (f32[13,512]{1,0:T(8,128)S(1)}, f32[13,512]{1,0:T(8,128)}, u32[]{:S(2)}) copy-start(f32[13,512]{1,0:T(8,128)} %param.27) | copy-start | bytes 79876
  169.5 5.6 %copy-start.16 = (f32[13,512]{1,0:T(8,128)S(1)}, f32[13,512]{1,0:T(8,128)}, u32[]{:S(2)}) copy-start(f32[13,512]{1,0:T(8,128)} %param.30) | copy-start | bytes 79876
  169.5 5.6 %copy-start.17 = (f32[13,512]{1,0:T(8,128)S(1)}, f32[13,512]{1,0:T(8,128)}, u32[]{:S(2)}) copy-start(f32[13,512]{1,0:T(8,128)} %param.33) | copy-start | bytes 79876
  175.8 10.8 %copy-start.14 = (f32[13,512]{1,0:T(8,128)}, f32[13,512]{1,0:T(8,128)S(1)}, u32[]{:S(2)}) copy-start(f32[13,512]{1,0:T(8,128)S(1)} %get-tuple-element.82) | copy-start | bytes 79876
  175.8 10.8 %copy-start.15 = (f32[13,512]{1,0:T(8,128)}, f32[13,512]{1,0:T(8,128)S(1)}, u32[]{:S(2)}) copy-start(f32[13,512]{1,0:T(8,128)S(1)} %get-tuple-element.83) | copy-start | bytes 79876
  179.4 7.1 %copy-start.4 = (f32[512,256]{1,0:T(8,128)}, f32[512,256]{1,0:T(8,128)S(1)}, u32[]{:S(2)}) copy-start(f32[512,256]{1,0:T(8,128)S(1)} %get-tuple-element.80) | copy-start | bytes 1572868
  179.4 7.1 %copy-start.5 = (f32[512,256]{1,0:T(8,128)}, f32[512,256]{1,0:T(8,128)S(1)}, u32[]{:S(2)}) copy-start(f32[512,256]{1,0:T(8,128)S(1)} %get-tuple-element.81) | copy-start | bytes 1572868
  182.7 3.9 %copy-start.11 = (f32[256,128]{1,0:T(8,128)}, f32[256,128]{1,0:T(8,128)S(1)}, u32[]{:S(2)}) copy-start(f32[256,128]{1,0:T(8,128)S(1)} %get-tuple-element.78) | copy-start | bytes 393220
  182.7 3.9 %copy-start.12 = (f32[256,128]{1,0:T(8,128)}, f32[256,128]{1,0:T(8,128)S(1)}, u32[]{:S(2)}) copy-start(f32[256,128]{1,0:T(8,128)S(1)} %get-tuple-element.79) | copy-start | bytes 393220
Sparse Core Ops, SparseCore 0:
  32.7 53.8 all-gather.1
